TPU v7x, 512 devices: a whole 4x8x8 slice. The times are simulated.
512 devices in a mesh: fsdp: 64 (over x, y, core), dp: 8 (over z).
Axes of the slice: x: 4, y: 8, z: 8, core: 2. Of those that a mesh axis runs over, the one named last changes fastest.
Arguments:
- grads: bfloat16 [8, 1024, 28672], P('dp', 'fsdp')
- block_slot: int32 [28], replicated, may hold values from 0 to 63, as said below
- left_stats: float32 [64, 1024, 1024], P('fsdp', 'dp')
- right_stats: float32 [64, 1024, 1024], P('fsdp', 'dp')
- left_root: bfloat16 [64, 1024, 1024], P('fsdp', 'dp')
- right_root: bfloat16 [64, 1024, 1024], P('fsdp', 'dp')
Outputs:
- left_new: float32 [64, 1024, 1024], P('fsdp', 'dp')
- right_new: float32 [64, 1024, 1024], P('fsdp', 'dp')
- update: bfloat16 [1024, 28672], P('fsdp')
Inputs may be any that keep to these rules, and one draw needn't show every extreme that they name: The entries of block_slot are distinct. Block b's statistics and roots sit in slot block_slot[b], which belongs to the fsdp device of index block_slot[b]; slots that no block names are empty and their statistics pass through unchanged.
All inputs are finite; a program needn't handle non-finite values.
Results may differ from a plain program's by a relative error of at most 0.015.
Values may be sent and summed in bfloat16 or wider, within the bound.
No kernel may reach another device: no remote copies, remote signals or barrier semaphores. Data moves between devices by JAX's collectives and lax.ppermute only.
A program may use at most 64 MiB of HBM per device.

v0:
```python
import jax
import jax.numpy as jnp
from jax import lax
from jax.sharding import Mesh
from jax.sharding import PartitionSpec as P

FSDP = ("fsdp_0", "fsdp_1", "fsdp_2")
epsilon = 1e-06


def split_terms(value):
    high = lax.reduce_precision(value, 8, 7)
    middle = lax.reduce_precision(value - high, 8, 7)
    low = value - high - middle
    return [term.astype(jnp.bfloat16) for term in (high, middle, low)]


def per_device(grads, block_slot, left_stats, right_stats, left_root, right_root):
    rows = grads[0]
    row_dev, col_count = rows.shape
    block_size = left_stats.shape[2]
    block_count = col_count // block_size
    shared = left_stats.shape[1]
    replicas = lax.axis_size("dp")
    total_slots = lax.axis_size(FSDP)
    slot_ids = jnp.arange(total_slots, dtype=jnp.int32)
    matches = block_slot[None, :] == slot_ids[:, None]
    filled = jnp.any(matches, axis=1)
    numbers = jnp.arange(block_count, dtype=jnp.int32)
    source = jnp.sum(jnp.where(matches, numbers[None, :], 0), axis=1)
    whole_left = lax.all_gather(left_root[0], "dp", axis=0, tiled=True)
    shares = rows.reshape(row_dev, block_count, replicas, shared).transpose(2, 1, 0, 3)
    shares = shares.reshape(replicas, block_count * row_dev, shared)
    roots = right_root[0].reshape(shared, replicas, shared).transpose(1, 0, 2)
    message = jnp.concatenate([shares, roots], axis=1)
    received = lax.all_to_all(message, "dp", 0, 0, tiled=True)
    summed = jnp.sum(received[:, : block_count * row_dev].astype(jnp.float32), axis=0)
    summed = summed.astype(jnp.bfloat16).reshape(block_count, row_dev, shared)
    right_cols = received[:, block_count * row_dev :]
    outgoing = jnp.where(
        filled[:, None, None], jnp.take(summed, source, axis=0), jnp.zeros((), jnp.bfloat16)
    )
    incoming = lax.all_to_all(outgoing, FSDP, 0, 0, tiled=True)
    mine, whole_left = lax.optimization_barrier((incoming.reshape(block_size, shared), whole_left))
    gradient = lax.all_gather(mine, "dp", axis=1, tiled=True)
    inner = jnp.einsum(
        "rk,kc->rc",
        gradient,
        right_cols.reshape(block_size, shared),
        preferred_element_type=jnp.float32,
    )
    high = lax.reduce_precision(inner, 8, 7)
    low = (inner - high).astype(jnp.bfloat16)
    high = high.astype(jnp.bfloat16)
    both = jnp.einsum(
        "kr,rc->kc", whole_left, high, preferred_element_type=jnp.float32
    ) + jnp.einsum("kr,rc->kc", whole_left, low, preferred_element_type=jnp.float32)
    partial = split_terms(jnp.sum(both * both))
    lanes = jnp.concatenate([jnp.stack(partial), jnp.zeros(shared - 3, jnp.bfloat16)])
    marks = jnp.broadcast_to(lanes[None, None, :], (total_slots, 8, shared))
    both = both.astype(jnp.bfloat16).reshape(total_slots, row_dev, shared)
    back = lax.all_to_all(jnp.concatenate([both, marks], axis=1), FSDP, 0, 0, tiled=True)
    row_start = lax.axis_index("dp") * shared
    own_rows = lax.dynamic_slice_in_dim(gradient, row_start, shared, 0)
    left_new = left_stats + jnp.einsum(
        "rc,kc->rk", own_rows, gradient, preferred_element_type=jnp.float32
    )
    right_new = right_stats + jnp.einsum(
        "rc,rk->ck", mine, gradient, preferred_element_type=jnp.float32
    )
    picked = jnp.take(back, block_slot, axis=0)
    terms = jnp.zeros((32, shared), jnp.bfloat16).at[:block_count].set(picked[:, row_dev, :])
    tiles = picked[:, :row_dev].reshape(block_count * row_dev, shared)
    gathered = lax.all_gather(jnp.concatenate([tiles, terms]), "dp", axis=0, tiled=False)
    full = gathered[:, : block_count * row_dev].reshape(replicas, block_count, row_dev, shared)
    terms = gathered[:, block_count * row_dev :][:, :block_count, :3].astype(jnp.float32)
    squares = jnp.sum(terms, axis=(0, 2))
    factor = lax.rsqrt(squares / (block_size * block_size) + epsilon)
    update = (full.astype(jnp.float32) * factor[None, :, None, None]).astype(jnp.bfloat16)
    update = update.transpose(2, 1, 0, 3).reshape(row_dev, col_count)
    return (left_new, right_new, update)


def solution(mesh):
    split = Mesh(
        mesh.devices.reshape(4, 8, 2, mesh.shape["dp"]), ("fsdp_0", "fsdp_1", "fsdp_2", "dp")
    )
    placed = (
        P("dp", FSDP, None),
        P(),
        P(FSDP, "dp", None),
        P(FSDP, "dp", None),
        P(FSDP, "dp", None),
        P(FSDP, "dp", None),
    )
    return jax.shard_map(
        per_device,
        mesh=split,
        in_specs=placed,
        out_specs=(P(FSDP, "dp", None), P(FSDP, "dp", None), P(FSDP, None)),
        check_vma=False,
    )
```

profile of v0, /device:TPU:8, one launch (start us, length us, event | category | flops | bytes accessed | tf_op | source)
XLA Modules:
  0.0 203.1 jit_solution(17511728519001342608)
XLA Ops:
  7.2 0.7 all-gather.7.cloned.1.call-update
  7.9 1.1 copy.15
  9.2 1.3 copy.19
  10.5 0.4 copy.14
  10.9 1.1 pad_maximum_fusion
  12.0 10.3 %all-to-all-start = ((bf16[8,576,128]{2,1,0:T(8,128)(2,1)}), bf16[8,576,128]{2,1,0:T(8,128)(2,1)S(1)}, u32[]{:S(2)}, u32[]{:S(2)}) async-start(bf16[8,576,128]{2,1,0:T(8,128)(2,1)} %pad_maximum_fusion), calls=%async_computation | async-start | bytes 2359296 | tf_op jit(solution)/shard_map/all_to_all | solution.py:36
  22.6 42.0 %all-to-all-done = bf16[8,576,128]{2,1,0:T(8,128)(2,1)S(1)} async-done(((bf16[8,576,128]{2,1,0:T(8,128)(2,1)}), bf16[8,576,128]{2,1,0:T(8,128)(2,1)S(1)}, u32[]{:S(2)}, u32[]{:S(2)}) %all-to-all-start) | async-done | bytes 1179680 | tf_op jit(solution)/shard_map/all_to_all | solution.py:36
  64.7 0.6 gather_fusion
  65.5 22.5 %all_to_all.15 = bf16[64,16,128]{2,1,0:T(8,128)(2,1)} all-to-all(bf16[64,16,128]{2,1,0:T(8,128)(2,1)S(1)} %select_select_fusion), channel_id=1, replica_groups=mesh['fsdp_0'=4,'fsdp_1'=8,'fsdp_2'=2,'dp'=8] {'fsdp_0','fsdp_1','fsdp_2'}, dimensions={0} | all-to-all | bytes 524288 | tf_op jit(solution)/shard_map/all_to_all | solution.py:43
  88.0 42.6 %all-gather.5.cloned.1.call-done = bf16[1024,1024]{1,0:T(8,128)(2,1)} async-done(((bf16[1024,128]{1,0:T(8,128)(2,1)}), bf16[1024,1024]{1,0:T(8,128)(2,1)}) %all-gather.5.cloned.1.call-update) | async-done | bytes 2097168 | tf_op jit(solution)/shard_map/all_gather | solution.py:45
  130.7 2.3 %fusion.14 = f32[1024,128]{1,0:T(8,128)S(1)} fusion(bf16[1024,1024]{1,0:T(8,128)(2,1)} %all-gather.5.cloned.1.call-done, bf16[1024,128]{1,0:T(8,128)(2,1)S(1)} %bitcast.64), kind=kOutput, calls=%fused_computation.42 | convolution fusion | flops 268435456 | bytes 2883584 | tf_op jit(solution)/shard_map/rk,kc->rc/dot_general | solution.py:46
  133.0 0.7 fusion.6
  133.7 0.9 copy-done.2
  134.6 1.3 fusion.13
  140.9 0.8 pad_maximum_fusion.1
  141.7 10.4 %all-to-all-start.2 = ((bf16[64,24,128]{2,1,0:T(8,128)(2,1)}), bf16[64,24,128]{2,1,0:T(8,128)(2,1)S(1)}, u32[]{:S(2)}, u32[]{:S(2)}) async-start(bf16[64,24,128]{2,1,0:T(8,128)(2,1)} %pad_maximum_fusion.1), calls=%async_computation.2 | async-start | bytes 786432 | tf_op jit(solution)/shard_map/all_to_all | solution.py:62
  152.2 1.6 fusion.1
  153.8 1.3 fusion.2
  155.1 11.5 %all-to-all-done.2 = bf16[64,24,128]{2,1,0:T(8,128)(2,1)S(1)} async-done(((bf16[64,24,128]{2,1,0:T(8,128)(2,1)}), bf16[64,24,128]{2,1,0:T(8,128)(2,1)S(1)}, u32[]{:S(2)}, u32[]{:S(2)}) %all-to-all-start.2) | async-done | bytes 393248 | tf_op jit(solution)/shard_map/all_to_all | solution.py:62
  166.5 0.6 gather_fusion.1
  167.3 26.6 %all-gather.1 = bf16[3840,128]{1,0:T(8,128)(2,1)S(1)} all-gather(bf16[480,128]{1,0:T(8,128)(2,1)S(1)} %fusion.9), channel_id=3, replica_groups=mesh['fsdp_0'=4,'fsdp_1'=8,'fsdp_2'=2,'dp'=8] {'dp'}, dimensions={0}, use_global_device_ids=true | all-gather | bytes 1105920 | tf_op jit(solution)/shard_map/all_gather | solution.py:74
  194.2 0.3 fusion.3
  194.4 0.6 copy.17
  195.0 1.3 copy.23
  (40 shorter events, 1.3 us)
Async XLA Ops:
  7.2 80.8 %all-gather.7.cloned.1.call-start = ((), (), s32[]{:S(2)}) async-start(), calls=%async_computation.4 | async-start | bytes 2359296 | tf_op jit(solution)/shard_map/all_gather | solution.py:31
  10.9 11.5 %copy-start.6 = (s32[28]{0:T(128)S(1)}, s32[28]{0:T(128)}, u32[]{:S(2)}) copy-start(s32[28]{0:T(128)} %param.9) | copy-start | bytes 340
  12.0 52.5 %all-to-all-start = ((bf16[8,576,128]{2,1,0:T(8,128)(2,1)}), bf16[8,576,128]{2,1,0:T(8,128)(2,1)S(1)}, u32[]{:S(2)}, u32[]{:S(2)}) async-start(bf16[8,576,128]{2,1,0:T(8,128)(2,1)} %pad_maximum_fusion), calls=%async_computation | async-start | bytes 2359296 | tf_op jit(solution)/shard_map/all_to_all | solution.py:36
  22.3 108.3 %all-gather.5.cloned.1.call-start = ((), (), s32[]{:S(2)}) async-start(), calls=%async_computation.3 | async-start | bytes 2359296 | tf_op jit(solution)/shard_map/all_gather | solution.py:45
  88.0 45.0 %copy-start.1 = (bf16[1,1024,1024]{2,1,0:T(8,128)(2,1)S(1)}, bf16[1,1024,1024]{2,1,0:T(8,128)(2,1)}, u32[]{:S(2)}) copy-start(bf16[1,1024,1024]{2,1,0:T(8,128)(2,1)} %all-gather.7.cloned.1.call-done) | copy-start | bytes 6291460
  133.0 1.6 copy-start.2
  134.6 17.6 %copy-start = (bf16[1024,1024]{1,0:T(8,128)(2,1)S(1)}, bf16[1024,1024]{1,0:T(8,128)(2,1)}, u32[]{:S(2)}) copy-start(bf16[1024,1024]{1,0:T(8,128)(2,1)} %all-gather.5.cloned.1.call-done) | copy-start | bytes 6291460
  134.6 17.6 %copy-start.4 = (f32[1,128,1024]{2,1,0:T(8,128)S(1)}, f32[1,128,1024]{2,1,0:T(8,128)}, u32[]{:S(2)}) copy-start(f32[1,128,1024]{2,1,0:T(8,128)} %param.10) | copy-start | bytes 1572868
  141.7 12.1 %copy-start.3 = (bf16[64,16,128]{2,1,0:T(8,128)(2,1)S(1)}, bf16[64,16,128]{2,1,0:T(8,128)(2,1)}, u32[]{:S(2)}) copy-start(bf16[64,16,128]{2,1,0:T(8,128)(2,1)} %all_to_all.15) | copy-start | bytes 786436
  141.7 24.8 %all-to-all-start.2 = ((bf16[64,24,128]{2,1,0:T(8,128)(2,1)}), bf16[64,24,128]{2,1,0:T(8,128)(2,1)S(1)}, u32[]{:S(2)}, u32[]{:S(2)}) async-start(bf16[64,24,128]{2,1,0:T(8,128)(2,1)} %pad_maximum_fusion.1), calls=%async_computation.2 | async-start | bytes 786432 | tf_op jit(solution)/shard_map/all_to_all | solution.py:62
  152.1 1.7 copy-start.5
Sparse Core Ops, SparseCore 0:
  10.1 64.5 all-gather.6
  88.1 42.4 all-gather.4
where the time goes:
time: 204 us; the launch traced here: 203 us
  waiting for transfers between devices  96.7 us (47%)
  blocking collectives  49.1 us (24%)
  starting transfers between devices  20.8 us (10%)
  between operations  19.2 us (9%)
  matrix products  7.21 us (4%)
  local copies, waits for them, and re-layouts  7.09 us (3%)
  other arithmetic  3.03 us (1%)
    all_gather x1, waiting for transfers between devices, per_device(): gradient = lax.all_gather(mine, 'dp', axis=1, tiled=True)  42.6 us
    all_to_all x1, waiting for transfers between devices, per_device(): received = lax.all_to_all(message, 'dp', 0, 0, tiled=True)  42 us
    all_gather x1, blocking collectives, per_device(): lax.all_gather(jnp.concatenate([tiles, terms]), 'dp', axis=0, tiled=False)  26.6 us
    all_to_all x1, blocking collectives, per_device(): incoming = lax.all_to_all(outgoing, FSDP, 0, 0, tiled=True)  22.5 us
    all_to_all x1, waiting for transfers between devices, per_device(): lax.all_to_all(jnp.concatenate([both, marks], axis=1), FSDP, 0, 0, tiled=...  11.5 us
    all_to_all x1, starting transfers between devices, per_device(): lax.all_to_all(jnp.concatenate([both, marks], axis=1), FSDP, 0, 0, tiled=...  10.4 us
    all_to_all x1, starting transfers between devices, per_device(): received = lax.all_to_all(message, 'dp', 0, 0, tiled=True)  10.3 us
    unnamed x18, local copies, waits for them, and re-layouts  4.61 us
  transfers between devices with their start and end apart: 4, of which 3 were waited for; matrix products, arithmetic and copies ran while one was open for 4% of the time, Pallas kernels for 0%

commit v1 on v0

--- a/solution.py
+++ b/solution.py
@@ -6,6 +6,28 @@
 
 FSDP = ("fsdp_0", "fsdp_1", "fsdp_2")
 epsilon = 1e-06
+
+
+def in_order(tiles, dim):
+    tiles = jnp.moveaxis(tiles, 0, dim)
+    lengths = tiles.shape
+    return tiles.reshape(*lengths[:dim], lengths[dim] * lengths[dim + 1], *lengths[dim + 2 :])
+
+
+def collect(x, axis, dim):
+    length = lax.axis_size(axis)
+    pairs = [(i, (i + 1) % length) for i in range(length)]
+    back = [(b, a) for a, b in pairs]
+    lower, upper = ([], [])
+    for lap in range(length - 1):
+        if lap % 2 == 0:
+            lower.append(lax.ppermute(lower[-1] if lower else x, axis, pairs))
+        else:
+            upper.append(lax.ppermute(upper[-1] if upper else x, axis, back))
+    pieces = jnp.stack([*lower[::-1], x, *upper])
+    shift = lax.axis_index(axis) - len(lower)
+    pieces = pieces[(jnp.arange(length) - shift) % length]
+    return in_order(pieces, dim)
 
 
 def split_terms(value):
@@ -42,7 +64,7 @@
     )
     incoming = lax.all_to_all(outgoing, FSDP, 0, 0, tiled=True)
     mine, whole_left = lax.optimization_barrier((incoming.reshape(block_size, shared), whole_left))
-    gradient = lax.all_gather(mine, "dp", axis=1, tiled=True)
+    gradient = collect(mine, "dp", 1)
     inner = jnp.einsum(
         "rk,kc->rc",
         gradient,

time: 204 us -> 203 us (level)
  waiting for transfers between devices: 96.7 us -> 66.8 us
  starting transfers between devices: 20.8 us -> 39.4 us
  local copies, waits for them, and re-layouts: 7.09 us -> 17 us
    all_gather x1 -> x0, waiting for transfers between devices: 42.6 us -> none  [per_device(): gradient = lax.all_gather(mine, 'dp', axis=1, tiled=True)]
    ppermute x0 -> x7, starting transfers between devices: none -> 23 us  [the longest x3 15.4 us: collect(): upper.append(lax.ppermute(upper[-1] if upper else x, axis, back))]
    ppermute x0 -> x7, waiting for transfers between devices: none -> 18.1 us  [the longest x4 18.1 us: collect(): lower.append(lax.ppermute(lower[-1] if lower else x, axis, pairs))]
    all_to_all x1, waiting for transfers between devices: 11.5 us -> 7.01 us  [per_device(): lax.all_to_all(jnp.concatenate([both, marks], axis=1), FSDP, 0, 0, tiled=...]
    all_to_all x1, starting transfers between devices: 10.4 us -> 6 us  [per_device(): lax.all_to_all(jnp.concatenate([both, marks], axis=1), FSDP, 0, 0, tiled=...]
    unnamed x18 -> x23, local copies, waits for them, and re-layouts: 4.61 us -> 8.69 us
    gather x0 -> x1, local copies, waits for them, and re-layouts: none -> 2.54 us  [collect(): pieces = pieces[(jnp.arange(length) - shift) % length]]
    transpose x1, local copies, waits for them, and re-layouts: 0.36 us -> 2.62 us  [in_order(): tiles = jnp.moveaxis(tiles, 0, dim)]
  transfers between devices with their start and end apart: 4 -> 10, of which waited for: 3 -> 6; matrix products, arithmetic and copies ran while one was open for 4% -> 8% of each run, Pallas kernels for 0% -> 0%
where the time goes in v1:
time: 203 us; the launch traced here: 202 us
  waiting for transfers between devices  66.8 us (33%)
  blocking collectives  49 us (24%)
  starting transfers between devices  39.4 us (19%)
  between operations  19.3 us (10%)
  local copies, waits for them, and re-layouts  17 us (8%)
  matrix products  7.46 us (4%)
  other arithmetic  3.04 us (1%)
    all_to_all x1, waiting for transfers between devices, per_device(): received = lax.all_to_all(message, 'dp', 0, 0, tiled=True)  41 us
    all_gather x1, blocking collectives, per_device(): lax.all_gather(jnp.concatenate([tiles, terms]), 'dp', axis=0, tiled=False)  26.6 us
    all_to_all x1, blocking collectives, per_device(): incoming = lax.all_to_all(outgoing, FSDP, 0, 0, tiled=True)  22.3 us
    ppermute x4, waiting for transfers between devices, collect(): lower.append(lax.ppermute(lower[-1] if lower else x, axis, pairs))  18.1 us
    ppermute x3, starting transfers between devices, collect(): upper.append(lax.ppermute(upper[-1] if upper else x, axis, back))  15.4 us
    all_to_all x1, starting transfers between devices, per_device(): received = lax.all_to_all(message, 'dp', 0, 0, tiled=True)  10.3 us
    unnamed x23, local copies, waits for them, and re-layouts  8.69 us
    ppermute x4, starting transfers between devices, collect(): lower.append(lax.ppermute(lower[-1] if lower else x, axis, pairs))  7.64 us
  transfers between devices with their start and end apart: 10, of which 6 were waited for; matrix products, arithmetic and copies ran while one was open for 8% of the time, Pallas kernels for 0%

profile of v1, /device:TPU:8, one launch (start us, length us, event | category | flops | bytes accessed | tf_op | source)
XLA Modules:
  0.0 202.0 jit_solution(14382854452556223865)
XLA Ops:
  7.9 1.3 copy.25
  11.1 10.3 %all-to-all-start = ((bf16[8,576,128]{2,1,0:T(8,128)(2,1)}), bf16[8,576,128]{2,1,0:T(8,128)(2,1)S(1)}, u32[]{:S(2)}, u32[]{:S(2)}) async-start(bf16[8,576,128]{2,1,0:T(8,128)(2,1)} %pad_maximum_fusion), calls=%async_computation | async-start | bytes 2359296 | tf_op jit(solution)/shard_map/all_to_all | solution.py:58
  21.6 41.0 %all-to-all-done = bf16[8,576,128]{2,1,0:T(8,128)(2,1)S(1)} async-done(((bf16[8,576,128]{2,1,0:T(8,128)(2,1)}), bf16[8,576,128]{2,1,0:T(8,128)(2,1)S(1)}, u32[]{:S(2)}, u32[]{:S(2)}) %all-to-all-start) | async-done | bytes 1179680 | tf_op jit(solution)/shard_map/all_to_all | solution.py:58
  63.5 22.3 %all_to_all.15 = bf16[64,16,128]{2,1,0:T(8,128)(2,1)S(1)} all-to-all(bf16[64,16,128]{2,1,0:T(8,128)(2,1)S(1)} %select_select_fusion), channel_id=1, replica_groups=mesh['fsdp_0'=4,'fsdp_1'=8,'fsdp_2'=2,'dp'=8] {'fsdp_0','fsdp_1','fsdp_2'}, dimensions={0} | all-to-all | bytes 524288 | tf_op jit(solution)/shard_map/all_to_all | solution.py:65
  85.9 1.9 collective-permute-start
  87.8 9.5 %collective-permute-done = bf16[1024,128]{1,0:T(8,128)(2,1)S(1)} collective-permute-done((bf16[1024,128]{1,0:T(8,128)(2,1)S(1)}, bf16[1024,128]{1,0:T(8,128)(2,1)S(1)}, u32[]{:S(2)}, u32[]{:S(2)}) %collective-permute-start) | collective-permute-done | bytes 262176 | tf_op jit(solution)/shard_map/ppermute | solution.py:24
  97.3 1.9 collective-permute-start.1
  99.3 5.1 %collective-permute-start.4 = (bf16[1024,128]{1,0:T(8,128)(2,1)S(1)}, bf16[1024,128]{1,0:T(8,128)(2,1)S(1)}, u32[]{:S(2)}, u32[]{:S(2)}) collective-permute-start(bf16[1024,128]{1,0:T(8,128)(2,1)S(1)} %bitcast.83), channel_id=1, source_target_pairs={{1,0},{2,1},{3,2},{4,3},{5,4},{6,5},{7,6},{0,7},{9,8},{10,9},{11,1... | collective-permute-start | bytes 786440 | tf_op jit(solution)/shard_map/ppermute | solution.py:26
  104.4 3.5 %collective-permute-done.1 = bf16[1024,128]{1,0:T(8,128)(2,1)S(1)} collective-permute-done((bf16[1024,128]{1,0:T(8,128)(2,1)S(1)}, bf16[1024,128]{1,0:T(8,128)(2,1)S(1)}, u32[]{:S(2)}, u32[]{:S(2)}) %collective-permute-start.1) | collective-permute-done | bytes 262176 | tf_op jit(solution)/shard_map/ppermute | solution.py:24
  107.9 1.9 collective-permute-start.2
  109.9 5.1 %collective-permute-start.5 = (bf16[1024,128]{1,0:T(8,128)(2,1)S(1)}, bf16[1024,128]{1,0:T(8,128)(2,1)S(1)}, u32[]{:S(2)}, u32[]{:S(2)}) collective-permute-start(bf16[1024,128]{1,0:T(8,128)(2,1)S(1)} %collective-permute-done.4), channel_id=1, source_target_pairs={{1,0},{2,1},{3,2},{4,3},{5,4},{6,5},{7,6},{0,7},{9,8},{10,9},{11,1... | collective-permute-start | bytes 786440 | tf_op jit(solution)/shard_map/ppermute | solution.py:26
  115.0 2.7 %collective-permute-done.2 = bf16[1024,128]{1,0:T(8,128)(2,1)S(1)} collective-permute-done((bf16[1024,128]{1,0:T(8,128)(2,1)S(1)}, bf16[1024,128]{1,0:T(8,128)(2,1)S(1)}, u32[]{:S(2)}, u32[]{:S(2)}) %collective-permute-start.2) | collective-permute-done | bytes 262176 | tf_op jit(solution)/shard_map/ppermute | solution.py:24
  117.7 1.9 collective-permute-start.3
  119.6 5.1 %collective-permute-start.6 = (bf16[1024,128]{1,0:T(8,128)(2,1)S(1)}, bf16[1024,128]{1,0:T(8,128)(2,1)S(1)}, u32[]{:S(2)}, u32[]{:S(2)}) collective-permute-start(bf16[1024,128]{1,0:T(8,128)(2,1)S(1)} %collective-permute-done.5), channel_id=1, source_target_pairs={{1,0},{2,1},{3,2},{4,3},{5,4},{6,5},{7,6},{0,7},{9,8},{10,9},{11,1... | collective-permute-start | bytes 786440 | tf_op jit(solution)/shard_map/ppermute | solution.py:26
  124.8 2.4 %collective-permute-done.3 = bf16[1024,128]{1,0:T(8,128)(2,1)S(1)} collective-permute-done((bf16[1024,128]{1,0:T(8,128)(2,1)S(1)}, bf16[1024,128]{1,0:T(8,128)(2,1)S(1)}, u32[]{:S(2)}, u32[]{:S(2)}) %collective-permute-start.3) | collective-permute-done | bytes 262176 | tf_op jit(solution)/shard_map/ppermute | solution.py:24
  132.9 2.5 %gather_fusion.1 = bf16[8,1024,128]{2,1,0:T(8,128)(2,1)S(1)} fusion(bf16[8,1024,128]{2,1,0:T(8,128)(2,1)} %bitcast_dynamic-update-slice_fusion, s32[1024]{0:T(1024)S(1)} %pad_clamp_fusion.1), kind=kCustom, calls=%fused_computation.1 | custom fusion | bytes 4194336 | tf_op jit(solution)/shard_map/gather | solution.py:29
  137.8 1.3 fusion.17
  144.9 6.0 %all-to-all-start.2 = ((bf16[64,24,128]{2,1,0:T(8,128)(2,1)}), bf16[64,24,128]{2,1,0:T(8,128)(2,1)S(1)}, u32[]{:S(2)}, u32[]{:S(2)}) async-start(bf16[64,24,128]{2,1,0:T(8,128)(2,1)} %pad_maximum_fusion.1), calls=%async_computation.2 | async-start | bytes 786432 | tf_op jit(solution)/shard_map/all_to_all | solution.py:84
  151.0 2.6 %copy.22 = bf16[1024,8,128]{0,2,1:T(8,128)(2,1)} copy(bf16[1024,8,128]{2,0,1:T(8,128)(2,1)S(1)} %bitcast.71) | data formatting | bytes 4194304 | tf_op jit(solution)/shard_map/transpose | solution.py:12
  153.6 3.1 %fusion.1 = f32[1,128,1024]{2,1,0:T(8,128)} fusion(f32[1,128,1024]{2,1,0:T(8,128)S(1)} %copy-done.2, bf16[1024,1024]{0,1:T(8,128)(2,1)} %bitcast.72, s32[]{:T(128)S(6)} %select_n.71), kind=kOutput, calls=%fused_computation.9 | convolution fusion | flops 268566528 | bytes 3407876 | tf_op jit(solution)/shard_map/rc,kc->rk/dot_general | solution.py:87
  156.7 1.6 fusion.2
  158.3 7.0 %all-to-all-done.2 = bf16[64,24,128]{2,1,0:T(8,128)(2,1)S(1)} async-done(((bf16[64,24,128]{2,1,0:T(8,128)(2,1)}), bf16[64,24,128]{2,1,0:T(8,128)(2,1)S(1)}, u32[]{:S(2)}, u32[]{:S(2)}) %all-to-all-start.2) | async-done | bytes 393248 | tf_op jit(solution)/shard_map/all_to_all | solution.py:84
  166.1 26.6 %all-gather.1 = bf16[3840,128]{1,0:T(8,128)(2,1)S(1)} all-gather(bf16[480,128]{1,0:T(8,128)(2,1)S(1)} %fusion.10), channel_id=3, replica_groups=mesh['fsdp_0'=4,'fsdp_1'=8,'fsdp_2'=2,'dp'=8] {'dp'}, dimensions={0}, use_global_device_ids=true | all-gather | bytes 1105920 | tf_op jit(solution)/shard_map/all_gather | solution.py:96
  193.8 1.3 copy.29
  (60 shorter events, 14.5 us)
Async XLA Ops:
  7.2 2.4 %copy-start.4 = (bf16[1,128,1024]{2,1,0:T(8,128)(2,1)S(1)}, bf16[1,128,1024]{2,1,0:T(8,128)(2,1)}, u32[]{:S(2)}) copy-start(bf16[1,128,1024]{2,1,0:T(8,128)(2,1)} %param.13) | copy-start | bytes 786436
  7.2 78.7 %all-gather.4.cloned.1.call-start = ((), (), s32[]{:S(2)}) async-start(), calls=%async_computation.3 | async-start | bytes 2359296 | tf_op jit(solution)/shard_map/all_gather | solution.py:53
  9.9 11.4 %copy-start.5 = (s32[28]{0:T(128)S(1)}, s32[28]{0:T(128)}, u32[]{:S(2)}) copy-start(s32[28]{0:T(128)} %param.9) | copy-start | bytes 340
  11.1 51.5 %all-to-all-start = ((bf16[8,576,128]{2,1,0:T(8,128)(2,1)}), bf16[8,576,128]{2,1,0:T(8,128)(2,1)S(1)}, u32[]{:S(2)}, u32[]{:S(2)}) async-start(bf16[8,576,128]{2,1,0:T(8,128)(2,1)} %pad_maximum_fusion), calls=%async_computation | async-start | bytes 2359296 | tf_op jit(solution)/shard_map/all_to_all | solution.py:58
  85.9 11.5 %collective-permute-start = (bf16[1024,128]{1,0:T(8,128)(2,1)S(1)}, bf16[1024,128]{1,0:T(8,128)(2,1)S(1)}, u32[]{:S(2)}, u32[]{:S(2)}) collective-permute-start(bf16[1024,128]{1,0:T(8,128)(2,1)S(1)} %bitcast.82), channel_id=1, source_target_pairs={{0,1},{1,2},{2,3},{3,4},{4,5},{5,6},{6,7},{7,0},{8,9},{9,10},{10,1... | collective-permute-start | bytes 786440 | tf_op jit(solution)/shard_map/ppermute | solution.py:24
  97.3 10.6 %collective-permute-start.1 = (bf16[1024,128]{1,0:T(8,128)(2,1)S(1)}, bf16[1024,128]{1,0:T(8,128)(2,1)S(1)}, u32[]{:S(2)}, u32[]{:S(2)}) collective-permute-start(bf16[1024,128]{1,0:T(8,128)(2,1)S(1)} %collective-permute-done), channel_id=1, source_target_pairs={{0,1},{1,2},{2,3},{3,4},{4,5},{5,6},{6,7},{7,0},{8,9},{9,10},{10,1... | collective-permute-start | bytes 786440 | tf_op jit(solution)/shard_map/ppermute | solution.py:24
  99.3 10.6 %collective-permute-start.4 = (bf16[1024,128]{1,0:T(8,128)(2,1)S(1)}, bf16[1024,128]{1,0:T(8,128)(2,1)S(1)}, u32[]{:S(2)}, u32[]{:S(2)}) collective-permute-start(bf16[1024,128]{1,0:T(8,128)(2,1)S(1)} %bitcast.83), channel_id=1, source_target_pairs={{1,0},{2,1},{3,2},{4,3},{5,4},{6,5},{7,6},{0,7},{9,8},{10,9},{11,1... | collective-permute-start | bytes 786440 | tf_op jit(solution)/shard_map/ppermute | solution.py:26
  107.9 9.8 %collective-permute-start.2 = (bf16[1024,128]{1,0:T(8,128)(2,1)S(1)}, bf16[1024,128]{1,0:T(8,128)(2,1)S(1)}, u32[]{:S(2)}, u32[]{:S(2)}) collective-permute-start(bf16[1024,128]{1,0:T(8,128)(2,1)S(1)} %collective-permute-done.1), channel_id=1, source_target_pairs={{0,1},{1,2},{2,3},{3,4},{4,5},{5,6},{6,7},{7,0},{8,9},{9,10},{10,1... | collective-permute-start | bytes 786440 | tf_op jit(solution)/shard_map/ppermute | solution.py:24
  109.9 9.7 %collective-permute-start.5 = (bf16[1024,128]{1,0:T(8,128)(2,1)S(1)}, bf16[1024,128]{1,0:T(8,128)(2,1)S(1)}, u32[]{:S(2)}, u32[]{:S(2)}) collective-permute-start(bf16[1024,128]{1,0:T(8,128)(2,1)S(1)} %collective-permute-done.4), channel_id=1, source_target_pairs={{1,0},{2,1},{3,2},{4,3},{5,4},{6,5},{7,6},{0,7},{9,8},{10,9},{11,1... | collective-permute-start | bytes 786440 | tf_op jit(solution)/shard_map/ppermute | solution.py:26
  117.7 9.5 %collective-permute-start.3 = (bf16[1024,128]{1,0:T(8,128)(2,1)S(1)}, bf16[1024,128]{1,0:T(8,128)(2,1)S(1)}, u32[]{:S(2)}, u32[]{:S(2)}) collective-permute-start(bf16[1024,128]{1,0:T(8,128)(2,1)S(1)} %collective-permute-done.2), channel_id=1, source_target_pairs={{0,1},{1,2},{2,3},{3,4},{4,5},{5,6},{6,7},{7,0},{8,9},{9,10},{10,1... | collective-permute-start | bytes 786440 | tf_op jit(solution)/shard_map/ppermute | solution.py:24
  119.6 12.6 %collective-permute-start.6 = (bf16[1024,128]{1,0:T(8,128)(2,1)S(1)}, bf16[1024,128]{1,0:T(8,128)(2,1)S(1)}, u32[]{:S(2)}, u32[]{:S(2)}) collective-permute-start(bf16[1024,128]{1,0:T(8,128)(2,1)S(1)} %collective-permute-done.5), channel_id=1, source_target_pairs={{1,0},{2,1},{3,2},{4,3},{5,4},{6,5},{7,6},{0,7},{9,8},{10,9},{11,1... | collective-permute-start | bytes 786440 | tf_op jit(solution)/shard_map/ppermute | solution.py:26
  135.5 1.6 copy-start.1
  144.9 20.4 %all-to-all-start.2 = ((bf16[64,24,128]{2,1,0:T(8,128)(2,1)}), bf16[64,24,128]{2,1,0:T(8,128)(2,1)S(1)}, u32[]{:S(2)}, u32[]{:S(2)}) async-start(bf16[64,24,128]{2,1,0:T(8,128)(2,1)} %pad_maximum_fusion.1), calls=%async_computation.2 | async-start | bytes 786432 | tf_op jit(solution)/shard_map/all_to_all | solution.py:84
  150.9 2.6 %copy-start.2 = (f32[1,128,1024]{2,1,0:T(8,128)S(1)}, f32[1,128,1024]{2,1,0:T(8,128)}, u32[]{:S(2)}) copy-start(f32[1,128,1024]{2,1,0:T(8,128)} %param.10) | copy-start | bytes 1572868
  153.6 3.1 %copy-start = (bf16[1024,8,128]{0,2,1:T(8,128)(2,1)S(1)}, bf16[1024,8,128]{0,2,1:T(8,128)(2,1)}, u32[]{:S(2)}) copy-start(bf16[1024,8,128]{0,2,1:T(8,128)(2,1)} %copy.22) | copy-start | bytes 6291460
  153.6 3.1 %copy-start.3 = (f32[1,128,1024]{2,1,0:T(8,128)S(1)}, f32[1,128,1024]{2,1,0:T(8,128)}, u32[]{:S(2)}) copy-start(f32[1,128,1024]{2,1,0:T(8,128)} %param.11) | copy-start | bytes 1572868
Sparse Core Ops, SparseCore 0:
  10.1 63.5 all-gather.3
